TPU v7x, 256 devices: a 2x2x32 block of a 4x8x32 slice. The times are simulated.
256 devices in a mesh: groups: 4 (over y, x), gx: 32 (over z), gy: 2 (over core).
Axes of the slice: x: 2, y: 2, z: 32, core: 2. Of those that a mesh axis runs over, the one named last changes fastest.
The devices are a block of a 4x8x32 slice.
Arguments:
- tokens: bfloat16 [2, 8192, 7168], P(None, ('groups', 'gx', 'gy')), parts along dimension 1, may hold values from -6 to 6
- expert_ids: int32 [2, 8192, 2], P(None, ('groups', 'gx', 'gy')), parts along dimension 1, may hold values from 0 to 15, all different within a row; in each aligned block of 32 rows (0 to 31, 32 to 63, ..., all dimensions but the last counted through in order) at most 6 rows name the same one
- gate_weights: float32 [2, 8192, 2], P(None, ('groups', 'gx', 'gy')), parts along dimension 1, may hold values from 0.1 to 1
- w_gate: bfloat16 [32, 7168, 512], P('gx', None, 'gy'), may hold values from -0.0625 to 0.0625
- w_up: bfloat16 [32, 7168, 512], P('gx', None, 'gy'), may hold values from -0.0625 to 0.0625
- w_down: bfloat16 [32, 512, 7168], P('gx', 'gy'), may hold values from -0.1875 to 0.1875
Outputs:
- combined: bfloat16 [2, 8192, 7168], P(None, ('groups', 'gx', 'gy')), parts along dimension 1
There are 4 independent parts, one for each index of `groups`. A program takes and returns all parts, laid end to end along the dimension named above; an argument that names none is the same for every part. Nothing has to cross between parts.
Inputs may be any that keep to these rules, and one draw needn't show every extreme that they name: `expert_ids`: each row names 2 different experts. Within the 32 rows of one device and one micro-batch no expert is named more than 6 times, and in some such blocks one is named exactly 6 times.
All inputs are finite; a program needn't handle non-finite values.
Results may differ from a plain program's by a relative error of at most 0.012.
Values may be sent and summed in bfloat16 or wider, within the bound.
A program may use at most 192 MiB of HBM per device.

v0:
```python
import jax
import jax.numpy as jnp
from jax import lax
from jax.sharding import PartitionSpec as P


def gather_turned(arrays, axis, dims):
    turned = [jnp.moveaxis(a, dim, 0) for a, dim in zip(arrays, dims)]
    both = jnp.concatenate([t.reshape(len(t), -1) for t in turned], axis=1)
    result, at, gathered = (lax.all_gather(both, axis, axis=0, tiled=True), 0, [])
    for t, dim in zip(turned, dims):
        share = result[:, at : at + t[0].size].reshape(-1, *t.shape[1:])
        gathered.append(jnp.moveaxis(share, 0, dim))
        at += t[0].size
    return tuple(gathered)


def in_blocks(value, dim, count):
    before, after = (value.shape[:dim], value.shape[dim + 1 :])
    return jnp.moveaxis(value.reshape(*before, count, -1, *after), dim, 0)


def cut_rows(length, count):
    unit = 8 if length >= 8 * count else 1
    return [length // unit * k // count * unit for k in range(1, count)]


def in_order(blocks, dim):
    blocks = jnp.moveaxis(blocks, 0, dim)
    dims = blocks.shape
    return blocks.reshape(*dims[:dim], dims[dim] * dims[dim + 1], *dims[dim + 2 :])


def several_exchanges(value, axis, pieces, split_dim, concat_dim):
    blocks = in_blocks(value, split_dim, lax.axis_size(axis))
    cut = max(range(1, max(2, blocks.ndim - 1)), key=lambda d: blocks.shape[d])
    gathered = []
    for share in jnp.split(blocks, cut_rows(blocks.shape[cut], pieces), axis=cut):
        if share.size:
            gathered.append(lax.all_to_all(share, axis, split_axis=0, concat_axis=0, tiled=True))
    return in_order(jnp.concatenate(gathered, axis=cut), concat_dim)


def swapped(value, axis, stride):
    return lax.ppermute(value, axis, [(i, i ^ 1 << stride) for i in range(lax.axis_size(axis))])


def slot_tables(chosen, gates, experts, capacity):
    rows, topk = chosen.shape
    flat = chosen.reshape(-1)
    marks = (flat[:, None] == jnp.arange(experts, dtype=jnp.int32)[None, :]).astype(jnp.int32)
    before = jnp.cumsum(marks, axis=0) - marks
    slot = jnp.sum(before * marks, axis=1)
    place = flat * capacity + slot
    table = (place[:, None] == jnp.arange(experts * capacity, dtype=jnp.int32)[None, :]).astype(
        jnp.float32
    )
    table = table.reshape(rows, topk, experts * capacity)
    picker = jnp.sum(table, axis=1)
    mixing = jnp.sum(table * gates[:, :, None], axis=1)
    return (picker, mixing)


def swiglu_part(slot_rows, wg, wu, wd):
    gate = jnp.dot(slot_rows, wg, preferred_element_type=jnp.float32)
    up = jnp.dot(slot_rows, wu, preferred_element_type=jnp.float32)
    hidden = (jax.nn.silu(gate) * up).astype(jnp.bfloat16)
    return jnp.dot(hidden, wd, preferred_element_type=jnp.float32).astype(jnp.bfloat16)


def body(tokens, expert_ids, gate_weights, w_gate, w_up, w_down):
    batches, rows, width = tokens.shape
    topk = expert_ids.shape[2]
    n_gx = lax.axis_size("gx")
    n_gy = lax.axis_size("gy")
    experts = n_gx // 2
    capacity = 2 * min(rows // 2, (5 * rows * topk + 8 * experts - 1) // (8 * experts))
    wg = w_gate[0]
    wu = w_up[0]
    wd = w_down[0]
    quarter = wg.shape[1]
    full_gate, full_up, full_down = gather_turned((wg, wu, wd), "gy", (1, 1, 0))
    parity = lax.axis_index("gx") % 2
    results = []
    for batch in range(batches):
        picker, mixing = slot_tables(expert_ids[batch], gate_weights[batch], experts, capacity)
        buffer = jnp.dot(
            picker.T.astype(jnp.bfloat16), tokens[batch], preferred_element_type=jnp.float32
        )
        buffer = buffer.astype(jnp.bfloat16).reshape(experts, capacity, width)
        outgoing = buffer.reshape(experts * 2, capacity // 2, width)
        own_half = several_exchanges(outgoing, "gx", 2, 0, 0)
        partner = swapped(own_half, "gx", 0)
        arrived = jnp.where(
            parity == 0,
            jnp.concatenate([own_half, partner], axis=1),
            jnp.concatenate([partner, own_half], axis=1),
        )
        slot_rows = arrived.reshape(-1, width)
        summed = jnp.zeros((slot_rows.shape[0], width), jnp.float32)
        for slice_index in range(n_gy):
            low = slice_index * quarter
            partial_value = swiglu_part(
                slot_rows,
                full_gate[:, low : low + quarter],
                full_up[:, low : low + quarter],
                full_down[low : low + quarter, :],
            )
            summed = summed + partial_value.astype(jnp.float32)
        half_rows = summed.astype(jnp.bfloat16).reshape(n_gx, capacity, width)
        returned = lax.all_to_all(half_rows, "gx", split_axis=0, concat_axis=0, tiled=True)
        expert_out = jnp.sum(
            returned.astype(jnp.float32).reshape(experts, 2, capacity, width), axis=1
        )
        expert_out = expert_out.reshape(experts * capacity, width)
        mixed = jnp.dot(
            mixing, expert_out, precision=lax.Precision.HIGHEST, preferred_element_type=jnp.float32
        )
        results.append(mixed.astype(jnp.bfloat16))
    return jnp.stack(results, axis=0)


def solution(mesh):
    placed = (
        P(None, ("groups", "gx", "gy"), None),
        P(None, ("groups", "gx", "gy"), None),
        P(None, ("groups", "gx", "gy"), None),
        P("gx", None, "gy"),
        P("gx", None, "gy"),
        P("gx", "gy", None),
    )
    return jax.shard_map(
        body,
        mesh=mesh,
        in_specs=placed,
        out_specs=P(None, ("groups", "gx", "gy"), None),
        check_vma=False,
    )
```

profile of v0, /device:TPU:46, one launch (start us, length us, event | category | flops | bytes accessed | tf_op | source)
XLA Modules:
  0.0 1218.1 jit_solution(2665821892989500899)
XLA Ops:
  6.6 5.9 copy.56
  12.5 5.9 copy.57
  18.4 11.5 pad_maximum_fusion
  34.8 3.3 reduce
  39.2 32.9 %all-to-all-start.3 = ((bf16[32,2,3584]{2,1,0:T(2,128)(2,1)}), bf16[32,2,3584]{2,1,0:T(2,128)(2,1)}, u32[]{:S(2)}, u32[]{:S(2)}) async-start(bf16[32,2,3584]{2,1,0:T(2,128)(2,1)} %reshape.98), calls=%async_computation.3 | async-start | bytes 917504 | tf_op jit(solution)/shard_map/all_to_all | solution.py:40
  78.5 3.3 reduce.1
  82.9 48.1 %all-to-all-done.3 = bf16[32,2,3584]{2,1,0:T(2,128)(2,1)} async-done(((bf16[32,2,3584]{2,1,0:T(2,128)(2,1)}), bf16[32,2,3584]{2,1,0:T(2,128)(2,1)}, u32[]{:S(2)}, u32[]{:S(2)}) %all-to-all-start.3) | async-done | bytes 458784 | tf_op jit(solution)/shard_map/all_to_all | solution.py:40
  131.0 4.8 all-to-all-start
  135.8 3.5 slice_bitcast_fusion.4
  139.3 54.6 %all-to-all-done = bf16[32,2,3584]{2,1,0:T(2,128)(2,1)S(1)} async-done(((bf16[32,2,3584]{2,1,0:T(2,128)(2,1)}), bf16[32,2,3584]{2,1,0:T(2,128)(2,1)S(1)}, u32[]{:S(2)}, u32[]{:S(2)}) %all-to-all-start) | async-done | bytes 458784 | tf_op jit(solution)/shard_map/all_to_all | solution.py:40
  193.8 4.8 all-to-all-start.1
  201.7 92.4 %all-to-all-done.1 = bf16[32,1,2,7168]{3,2,1,0:T(2,128)(2,1)S(1)} async-done(((bf16[32,1,2,7168]{3,2,1,0:T(2,128)(2,1)}), bf16[32,1,2,7168]{3,2,1,0:T(2,128)(2,1)S(1)}, u32[]{:S(2)}, u32[]{:S(2)}) %all-to-all-start.1) | async-done | bytes 917536 | tf_op jit(solution)/shard_map/all_to_all | solution.py:40
  294.1 5.5 all-to-all-start.4
  305.7 101.5 %collective-permute-done = bf16[32,3,7168]{2,0,1:T(8,128)(2,1)S(1)} collective-permute-done((bf16[32,3,7168]{2,0,1:T(8,128)(2,1)}, bf16[32,3,7168]{2,0,1:T(8,128)(2,1)S(1)}, u32[]{:S(2)}, u32[]{:S(2)}) %collective-permute-start) | collective-permute-done | bytes 1376288 | tf_op jit(solution)/shard_map/ppermute | solution.py:45
  408.3 4.5 maximum_select_fusion
  416.0 8.4 slice_bitcast_fusion.1
  428.8 9.0 fusion.7
  437.8 9.7 fusion.6
  447.5 4.7 reshape.85
  452.2 21.2 %all-to-all-start.2 = ((bf16[32,6,7168]{2,1,0:T(8,128)(2,1)}), bf16[32,6,7168]{2,1,0:T(8,128)(2,1)}, u32[]{:S(2)}, u32[]{:S(2)}) async-start(bf16[32,6,7168]{2,1,0:T(8,128)(2,1)} %reshape.85), calls=%async_computation.2 | async-start | bytes 7340032 | tf_op jit(solution)/shard_map/all_to_all | solution.py:111
  481.4 337.5 %collective-permute-done.1 = bf16[32,3,7168]{2,0,1:T(8,128)(2,1)S(1)} collective-permute-done((bf16[32,3,7168]{2,0,1:T(8,128)(2,1)S(1)}, bf16[32,3,7168]{2,0,1:T(8,128)(2,1)S(1)}, u32[]{:S(2)}, u32[]{:S(2)}) %collective-permute-start.1) | collective-permute-done | bytes 1376288 | tf_op jit(solution)/shard_map/ppermute | solution.py:45
  820.1 4.5 maximum_select_fusion.1
  827.8 3.4 fusion.22
  831.2 3.4 fusion.12
  834.6 9.0 fusion.3
  843.6 9.7 fusion.2
  853.3 4.6 reshape.90
  857.9 21.4 %all-to-all-start.5 = ((bf16[32,6,7168]{2,1,0:T(8,128)(2,1)}), bf16[32,6,7168]{2,1,0:T(8,128)(2,1)}, u32[]{:S(2)}, u32[]{:S(2)}) async-start(bf16[32,6,7168]{2,1,0:T(8,128)(2,1)} %reshape.90), calls=%async_computation.5 | async-start | bytes 7340032 | tf_op jit(solution)/shard_map/all_to_all | solution.py:111
  879.4 5.2 convert_reduce_fusion.1
  886.8 311.5 %all-to-all-done.5 = bf16[32,6,7168]{2,1,0:T(8,128)(2,1)} async-done(((bf16[32,6,7168]{2,1,0:T(8,128)(2,1)}), bf16[32,6,7168]{2,1,0:T(8,128)(2,1)}, u32[]{:S(2)}, u32[]{:S(2)}) %all-to-all-start.5) | async-done | bytes 2752544 | tf_op jit(solution)/shard_map/all_to_all | solution.py:111
  1198.4 5.1 convert_reduce_fusion
  1203.4 3.4 reshape.93
  (61 shorter events, 50.1 us)
Async XLA Ops:
  6.5 409.5 %all-gather.2.cloned.1.call-start = ((), (), s32[]{:S(2)}) async-start(), calls=%async_computation.6 | async-start | bytes 33030144 | tf_op jit(solution)/shard_map/all_gather | solution.py:10
  29.9 0.7 copy-start.3
  29.9 2.2 copy-start.4
  29.9 2.3 copy-start.2
  39.2 91.8 %all-to-all-start.3 = ((bf16[32,2,3584]{2,1,0:T(2,128)(2,1)}), bf16[32,2,3584]{2,1,0:T(2,128)(2,1)}, u32[]{:S(2)}, u32[]{:S(2)}) async-start(bf16[32,2,3584]{2,1,0:T(2,128)(2,1)} %reshape.98), calls=%async_computation.3 | async-start | bytes 917504 | tf_op jit(solution)/shard_map/all_to_all | solution.py:40
  131.0 62.9 %all-to-all-start = ((bf16[32,2,3584]{2,1,0:T(2,128)(2,1)}), bf16[32,2,3584]{2,1,0:T(2,128)(2,1)S(1)}, u32[]{:S(2)}, u32[]{:S(2)}) async-start(bf16[32,2,3584]{2,1,0:T(2,128)(2,1)} %reshape.100), calls=%async_computation | async-start | bytes 917504 | tf_op jit(solution)/shard_map/all_to_all | solution.py:40
  193.8 100.2 %all-to-all-start.1 = ((bf16[32,1,2,7168]{3,2,1,0:T(2,128)(2,1)}), bf16[32,1,2,7168]{3,2,1,0:T(2,128)(2,1)S(1)}, u32[]{:S(2)}, u32[]{:S(2)}) async-start(bf16[32,1,2,7168]{3,2,1,0:T(2,128)(2,1)} %slice_bitcast_fusion.4), calls=%async_computation.1 | async-start | bytes 1835008 | tf_op jit(solution)/shard_map/all_to_all | solution.py:40
  294.1 158.1 %all-to-all-start.4 = ((bf16[32,1,2,7168]{3,2,1,0:T(2,128)(2,1)}), bf16[32,1,2,7168]{3,2,1,0:T(2,128)(2,1)}, u32[]{:S(2)}, u32[]{:S(2)}) async-start(bf16[32,1,2,7168]{3,2,1,0:T(2,128)(2,1)} %slice_bitcast_fusion.2), calls=%async_computation.4 | async-start | bytes 1835008 | tf_op jit(solution)/shard_map/all_to_all | solution.py:40
  304.3 102.8 %collective-permute-start = (bf16[32,3,7168]{2,0,1:T(8,128)(2,1)}, bf16[32,3,7168]{2,0,1:T(8,128)(2,1)S(1)}, u32[]{:S(2)}, u32[]{:S(2)}) collective-permute-start(bf16[32,3,7168]{2,0,1:T(8,128)(2,1)} %copy.53), channel_id=1, source_target_pairs={{0,2},{2,0},{4,6},{6,4},{8,10},{10,8},{12,14},{14,12},{16,18},{18,... | collective-permute-start | bytes 4128776 | tf_op jit(solution)/shard_map/ppermute | solution.py:45
  424.5 3.0 copy-start.1
  452.2 405.8 %all-to-all-start.2 = ((bf16[32,6,7168]{2,1,0:T(8,128)(2,1)}), bf16[32,6,7168]{2,1,0:T(8,128)(2,1)}, u32[]{:S(2)}, u32[]{:S(2)}) async-start(bf16[32,6,7168]{2,1,0:T(8,128)(2,1)} %reshape.85), calls=%async_computation.2 | async-start | bytes 7340032 | tf_op jit(solution)/shard_map/all_to_all | solution.py:111
  480.0 338.9 %collective-permute-start.1 = (bf16[32,3,7168]{2,0,1:T(8,128)(2,1)S(1)}, bf16[32,3,7168]{2,0,1:T(8,128)(2,1)S(1)}, u32[]{:S(2)}, u32[]{:S(2)}) collective-permute-start(bf16[32,3,7168]{2,0,1:T(8,128)(2,1)S(1)} %copy.64), channel_id=1, source_target_pairs={{0,2},{2,0},{4,6},{6,4},{8,10},{10,8},{12,14},{14,12},{16,18},{18,... | collective-permute-start | bytes 4128776 | tf_op jit(solution)/shard_map/ppermute | solution.py:45
  857.9 340.4 %all-to-all-start.5 = ((bf16[32,6,7168]{2,1,0:T(8,128)(2,1)}), bf16[32,6,7168]{2,1,0:T(8,128)(2,1)}, u32[]{:S(2)}, u32[]{:S(2)}) async-start(bf16[32,6,7168]{2,1,0:T(8,128)(2,1)} %reshape.90), calls=%async_computation.5 | async-start | bytes 7340032 | tf_op jit(solution)/shard_map/all_to_all | solution.py:111
  1206.8 1.8 copy-start
Sparse Core Ops, SparseCore 0:
  30.1 64.8 all-gather.1
where the time goes:
time: 1230 us; the launch traced here: 1220 us
  waiting for transfers between devices  946 us (77%)
  starting transfers between devices  93.4 us (8%)
  local copies, waits for them, and re-layouts  67.9 us (6%)
  matrix products  52 us (4%)
  other arithmetic  45.3 us (4%)
  between operations  13.9 us (1%)
    ppermute x2, waiting for transfers between devices, swapped(): lax.ppermute(value, axis, [(i, i ^ 1 << stride) for i in range(lax.axis_s...  439 us
    all_to_all x2, waiting for transfers between devices, body(): lax.all_to_all(half_rows, 'gx', split_axis=0, concat_axis=0, tiled=True)  312 us
    all_to_all x4, waiting for transfers between devices, several_exchanges(): lax.all_to_all(share, axis, split_axis=0, concat_axis=0, tiled=True)  195 us
    all_to_all x4, starting transfers between devices, several_exchanges(): lax.all_to_all(share, axis, split_axis=0, concat_axis=0, tiled=True)  47.9 us
    all_to_all x2, starting transfers between devices, body(): lax.all_to_all(half_rows, 'gx', split_axis=0, concat_axis=0, tiled=True)  42.7 us
    dot_general x4, matrix products, swiglu_part(): jnp.dot(hidden, wd, preferred_element_type=jnp.float32).astype(jnp.bfloat16)  37.4 us
  transfers between devices with their start and end apart: 9, of which 6 were waited for; matrix products, arithmetic and copies ran while one was open for 10% of the time, Pallas kernels for 0%

commit v1 on v0

v1 whole, which is shorter than its diff:
```python
import functools

import jax
import jax.numpy as jnp
from jax import lax
from jax.experimental import pallas as pl
from jax.experimental.pallas import tpu as pltpu
from jax.sharding import PartitionSpec as P

MESH = pl.DeviceIdType.MESH
CHUNKS = 4
GROUP = 16


class Ring:
    def __init__(self, n, batches, rows, capacity):
        self.n = n
        self.hops = n // 2
        self.whole = n // 4
        self.experts = n // 2
        self.batches = batches
        self.tokens = batches * rows
        self.capacity = capacity
        self.used = batches * capacity
        assert self.used <= GROUP

    def listed(self, hop):
        return (self.hops - hop) // 2 + 1

    def sent(self, hop):
        if hop <= self.whole:
            return self.tokens
        return -(-self.listed(hop) * self.used // 8) * 8

    @property
    def most(self):
        return self.sent(self.whole + 1)

    def place(self, me, way):
        return me if way == 0 else self.n - 1 - me

    def source(self, me, way, hop):
        return lax.rem(self.place(me, way) - hop + self.n, self.n)

    def first(self, me, way, hop):
        start = self.source(me, way, hop)
        return (start + self.hops - 1) // 2 - (start + hop) // 2

    def group(self, way, hop):
        if hop == self.hops or way == 0:
            return hop
        return self.hops + hop

    def target(self, row, expert):
        batch = jnp.zeros_like(row)
        for b in range(1, self.batches):
            batch = batch + (row >= b * self.capacity).astype(jnp.int32)
        key = batch * (self.experts * self.capacity - self.capacity) + row + expert * self.capacity
        return jnp.where(row < self.used, key, -1).astype(jnp.float32)

    def list_target(self, row, me, way, hop):
        start = self.source(me, way, hop)
        last = lax.rem((start + self.hops - 1) // 2, self.experts)
        at = jnp.zeros_like(row)
        for k in range(1, self.listed(self.whole + 1)):
            at = at + (row >= k * self.used).astype(jnp.int32)
        expert = last - at
        expert = jnp.where(expert < 0, expert + self.experts, expert)
        if way == 1:
            expert = self.experts - 1 - expert
        row = row - at * self.used
        return jnp.where(
            at < self.listed(self.whole + 1), self.target(row, expert), -1.0
        )


def iota(shape, dim):
    return lax.broadcasted_iota(jnp.int32, shape, dim)


def enter(right, left):
    barrier = pltpu.get_barrier_semaphore()
    for neighbour in (left, right):
        pl.semaphore_signal(barrier, inc=1, device_id={"gx": neighbour}, device_id_type=MESH)
    pl.semaphore_wait(barrier, 2)


def columns(c, width):
    return pl.ds(c * width, width)


def dispatch_kernel(ring, x_ref, meta_ref, rows_ref, metas_ref, tok, slots, conv,
                    send_sem, recv_sem, meta_send, meta_recv):
    n, hops, whole = ring.n, ring.hops, ring.whole
    me = lax.axis_index("gx")
    right, left = lax.rem(me + 1, n), lax.rem(me + n - 1, n)
    width = x_ref.shape[1]
    part = width // CHUNKS
    expert = me // 2

    def held(way, hop):
        if hop == 0:
            return x_ref
        if hop <= whole:
            return tok.at[way, hop - 1]
        return slots.at[way, hop - whole - 1]

    def copy(way, hop, c):
        source = conv.at[way] if hop == whole + 1 else held(way, hop - 1)
        rows = pl.ds(0, ring.sent(hop))
        return pltpu.make_async_remote_copy(
            src_ref=source.at[rows, columns(c, part)],
            dst_ref=held(way, hop).at[rows, columns(c, part)],
            send_sem=send_sem.at[way, hop - 1, c],
            recv_sem=recv_sem.at[way, hop - 1, c],
            device_id={"gx": left if way else right},
            device_id_type=MESH,
        )

    def meta_copy(way, hop):
        return pltpu.make_async_remote_copy(
            src_ref=meta_ref if hop == 1 else metas_ref.at[way, hop - 2],
            dst_ref=metas_ref.at[way, hop - 1],
            send_sem=meta_send.at[way, hop - 1],
            recv_sem=meta_recv.at[way, hop - 1],
            device_id={"gx": left if way else right},
            device_id_type=MESH,
        )

    def picker(meta, target):
        keys = [meta[k : k + 1, : ring.tokens] for k in range(2)]
        hit = (keys[0] == target) | (keys[1] == target)
        return hit.astype(jnp.float32).astype(jnp.bfloat16)

    def spread(parts, group):
        @pl.loop(0, CHUNKS)
        def _(c):
            at = pl.ds(pl.multiple_of(c * part, 128), part)
            total = None
            for pick, block, count in parts:
                value = jnp.dot(pick, block[pl.ds(0, count), at], preferred_element_type=jnp.float32)
                total = value if total is None else total + value
            rows_ref[pl.ds(group * GROUP, GROUP), at] = total.astype(jnp.bfloat16)

    own_target = ring.target(iota((GROUP, 1), 0), expert)

    enter(right, left)
    for way in range(2):
        meta_copy(way, 1).start()
    for c in range(CHUNKS):
        for way in range(2):
            copy(way, 1, c).start()
    spread([(picker(meta_ref[...], own_target), x_ref, ring.tokens)], 0)

    for hop in range(1, hops + 1):
        for way in range(2):
            meta_copy(way, hop).wait_recv()
            if hop < hops:
                meta_copy(way, hop + 1).start()
        if hop == whole:
            pickers = [
                picker(
                    metas_ref[way, hop - 1],
                    ring.list_target(iota((ring.most, 1), 0), me, way, hop),
                )
                for way in range(2)
            ]
        for c in range(CHUNKS):
            for way in range(2):
                copy(way, hop, c).wait_recv()
                if hop == whole:
                    conv[way, :, columns(c, part)] = jnp.dot(
                        pickers[way],
                        tok[way, whole - 1, :, columns(c, part)],
                        preferred_element_type=jnp.float32,
                    ).astype(jnp.bfloat16)
                if hop < hops:
                    copy(way, hop + 1, c).start()
        parts = []
        for way in range(2):
            if hop <= whole:
                pick = picker(metas_ref[way, hop - 1], own_target)
            else:
                first = ring.first(me, way, hop)
                shape = (GROUP, ring.sent(hop))
                row, col = iota(shape, 0), iota(shape, 1)
                hit = (col == first * ring.used + row) & (row < ring.used) & (row >= -first * GROUP)
                pick = hit.astype(jnp.float32).astype(jnp.bfloat16)
            parts.append((pick, held(way, hop), ring.sent(hop)))
        if hop == hops:
            spread(parts, hop)
        else:
            for way in range(2):
                spread(parts[way : way + 1], ring.group(way, hop))

    for hop in range(1, hops + 1):
        for way in range(2):
            meta_copy(way, hop).wait_send()
            for c in range(CHUNKS):
                copy(way, hop, c).wait_send()


def return_kernel(ring, y_ref, metas_ref, out_ref, tok, slots, turn, last, send_sem, recv_sem):
    n, hops, whole = ring.n, ring.hops, ring.whole
    me = lax.axis_index("gx")
    right, left = lax.rem(me + 1, n), lax.rem(me + n - 1, n)
    width = out_ref.shape[1]
    part = width // CHUNKS
    expert = me // 2

    def held(way, hop):
        if hop < whole:
            return tok.at[way, hop]
        if hop < hops:
            return slots.at[way, hop - whole]
        return last.at[way]

    def copy(way, hop, c):
        rows = pl.ds(0, ring.sent(hop))
        source = turn.at[way] if hop == whole else held(way, hop)
        return pltpu.make_async_remote_copy(
            src_ref=source.at[rows, columns(c, part)],
            dst_ref=held(way, hop - 1).at[rows, columns(c, part)],
            send_sem=send_sem.at[way, hop - 1, c],
            recv_sem=recv_sem.at[way, hop - 1, c],
            device_id={"gx": right if way else left},
            device_id_type=MESH,
        )

    def mixer(at, target):
        meta = metas_ref[at]
        mix = jnp.zeros((ring.tokens, target.shape[1]), jnp.float32)
        for k in range(2):
            mix = mix + jnp.where(meta[:, k : k + 1] == target, meta[:, 2 + k : 3 + k], 0.0)
        high = mix.astype(jnp.bfloat16)
        return high, (mix - high.astype(jnp.float32)).astype(jnp.bfloat16)

    def mixed(pair, rows):
        return jnp.dot(pair[0], rows, preferred_element_type=jnp.float32) + jnp.dot(
            pair[1], rows, preferred_element_type=jnp.float32
        )

    def own_rows(way, hop, c):
        return y_ref[pl.ds(ring.group(way, hop) * GROUP, GROUP), columns(c, part)]

    def placer(way, hop):
        first = ring.first(me, way, hop)
        shape = (ring.sent(hop), GROUP)
        row, col = iota(shape, 0), iota(shape, 1)
        hit = (row == first * ring.used + col) & (col < ring.used) & (col >= -first * GROUP)
        return hit.astype(jnp.float32).astype(jnp.bfloat16)

    for hop in range(whole + 1, hops):
        more, had = ring.sent(hop), ring.sent(hop + 1)
        if more > had:
            for way in range(2):
                slots[way, hop - whole, pl.ds(had, more - had), :] = jnp.zeros(
                    (more - had, width), jnp.bfloat16
                )

    enter(right, left)
    own_target = ring.target(iota((1, GROUP), 1), expert)
    for hop in range(hops, 0, -1):
        count = ring.sent(hop)
        if hop > whole:
            tables = [placer(way, hop) for way in range(2)]
        else:
            tables = [mixer(way * (whole + 1) + hop, own_target) for way in range(2)]
        if hop == whole:
            lists = [
                mixer(
                    way * (whole + 1) + hop,
                    ring.list_target(iota((1, ring.most), 1), me, way, hop),
                )
                for way in range(2)
            ]
        for c in range(CHUNKS):
            for way in range(2):
                at = columns(c, part)
                if hop < hops:
                    copy(way, hop + 1, c).wait_recv()
                rows = own_rows(way, hop, c)
                if hop > whole:
                    value = jnp.dot(tables[way], rows, preferred_element_type=jnp.float32)
                    if hop == hops:
                        last[way, :, at] = value.astype(jnp.bfloat16)
                    else:
                        have = slots[way, hop - whole, pl.ds(0, count), at]
                        slots[way, hop - whole, pl.ds(0, count), at] = (
                            value + have.astype(jnp.float32)
                        ).astype(jnp.bfloat16)
                elif hop == whole:
                    value = mixed(tables[way], rows) + mixed(lists[way], slots[way, 0, :, at])
                    turn[way, :, at] = value.astype(jnp.bfloat16)
                else:
                    value = mixed(tables[way], rows) + tok[way, hop, :, at].astype(jnp.float32)
                    tok[way, hop, :, at] = value.astype(jnp.bfloat16)
                copy(way, hop, c).start()
    own = mixer(0, own_target)
    for c in range(CHUNKS):
        at = columns(c, part)
        value = mixed(own, own_rows(0, 0, c))
        for way in range(2):
            copy(way, 1, c).wait_recv()
            value = value + tok[way, 0, :, at].astype(jnp.float32)
        out_ref[:, at] = value.astype(jnp.bfloat16)
    for hop in range(1, hops + 1):
        for way in range(2):
            for c in range(CHUNKS):
                copy(way, hop, c).wait_send()


def vmem(count=1):
    return [pl.BlockSpec(memory_space=pltpu.VMEM)] * count


def dispatch(ring, tokens, meta):
    width = tokens.shape[1]
    groups = ring.n
    hops, whole = ring.hops, ring.whole
    sems = pltpu.SemaphoreType.DMA
    sent = sum(ring.sent(hop) for hop in range(1, hops + 1)) * width * 4
    return pl.pallas_call(
        functools.partial(dispatch_kernel, ring),
        out_shape=(
            jax.ShapeDtypeStruct((groups * GROUP, width), jnp.bfloat16),
            jax.ShapeDtypeStruct((2, hops, 8, 128), jnp.float32),
        ),
        in_specs=vmem(2),
        out_specs=tuple(vmem(2)),
        scratch_shapes=[
            pltpu.VMEM((2, whole, ring.tokens, width), jnp.bfloat16),
            pltpu.VMEM((2, hops - whole, ring.most, width), jnp.bfloat16),
            pltpu.VMEM((2, ring.most, width), jnp.bfloat16),
            sems((2, hops, CHUNKS)),
            sems((2, hops, CHUNKS)),
            sems((2, hops)),
            sems((2, hops)),
        ],
        compiler_params=pltpu.CompilerParams(collective_id=0, has_side_effects=True),
        cost_estimate=pl.CostEstimate(
            flops=4 * groups * GROUP * 64 * width, bytes_accessed=20 * sent, transcendentals=0
        ),
        name="dispatch",
    )(tokens, meta)


def give_back(ring, values, metas, width):
    hops, whole = ring.hops, ring.whole
    sems = pltpu.SemaphoreType.DMA
    sent = sum(ring.sent(hop) for hop in range(1, hops + 1)) * width * 4
    return pl.pallas_call(
        functools.partial(return_kernel, ring),
        out_shape=jax.ShapeDtypeStruct((ring.tokens, width), jnp.bfloat16),
        in_specs=vmem(2),
        out_specs=vmem()[0],
        scratch_shapes=[
            pltpu.VMEM((2, whole, ring.tokens, width), jnp.bfloat16),
            pltpu.VMEM((2, hops - whole, ring.most, width), jnp.bfloat16),
            pltpu.VMEM((2, ring.tokens, width), jnp.bfloat16),
            pltpu.VMEM((2, ring.sent(hops), width), jnp.bfloat16),
            sems((2, hops, CHUNKS)),
            sems((2, hops, CHUNKS)),
        ],
        compiler_params=pltpu.CompilerParams(collective_id=1, has_side_effects=True),
        cost_estimate=pl.CostEstimate(
            flops=4 * ring.n * GROUP * 64 * width, bytes_accessed=20 * sent, transcendentals=0
        ),
        name="give_back",
    )(values, metas)


def slot_keys(expert_ids, ring):
    batches, rows, topk = expert_ids.shape
    flat = expert_ids.reshape(batches, rows * topk)
    earlier = jnp.tril(jnp.ones((rows * topk, rows * topk), jnp.bool_), -1)
    same = flat[:, :, None] == flat[:, None, :]
    slot = jnp.sum((same & earlier[None]).astype(jnp.int32), axis=2)
    key = flat * ring.capacity + slot
    key = key + jnp.arange(batches, dtype=jnp.int32)[:, None] * (ring.experts * ring.capacity)
    return key.reshape(batches * rows, topk).astype(jnp.float32)


def body(tokens, expert_ids, gate_weights, w_gate, w_up, w_down):
    batches, rows, width = tokens.shape
    topk = expert_ids.shape[2]
    n = lax.axis_size("gx")
    experts = n // 2
    capacity = 2 * min(rows // 2, (5 * rows * topk + 8 * experts - 1) // (8 * experts))
    ring = Ring(n, batches, rows, capacity)

    keys = slot_keys(expert_ids, ring)
    gates = gate_weights.reshape(batches * rows, topk)
    both = jnp.concatenate([keys, gates], axis=1)
    meta = jnp.pad(both.T, ((0, 8 - 2 * topk), (0, 128 - batches * rows)))

    full_gate = lax.all_gather(w_gate[0], "gy")
    full_up = lax.all_gather(w_up[0], "gy")
    full_down = lax.all_gather(w_down[0], "gy")

    slot_rows, metas = dispatch(ring, tokens.reshape(batches * rows, width), meta)

    values = jnp.zeros((slot_rows.shape[0], width), jnp.float32)
    for q in range(full_gate.shape[0]):
        gate = jnp.dot(slot_rows, full_gate[q], preferred_element_type=jnp.float32)
        up = jnp.dot(slot_rows, full_up[q], preferred_element_type=jnp.float32)
        hidden = (jax.nn.silu(gate) * up).astype(jnp.bfloat16)
        values = values + jnp.dot(hidden, full_down[q], preferred_element_type=jnp.float32)
    values = values.astype(jnp.bfloat16)

    near = jnp.swapaxes(metas[:, : ring.whole, : 2 * topk, : ring.tokens], 2, 3)
    near = jnp.concatenate([jnp.broadcast_to(both, (2, 1, *both.shape)), near], axis=1)
    near = near.reshape(-1, *both.shape)
    out = give_back(ring, values, near, width)
    return out.reshape(batches, rows, width)


def solution(mesh):
    placed = (
        P(None, ("groups", "gx", "gy"), None),
        P(None, ("groups", "gx", "gy"), None),
        P(None, ("groups", "gx", "gy"), None),
        P("gx", None, "gy"),
        P("gx", None, "gy"),
        P("gx", "gy", None),
    )
    return jax.shard_map(
        body,
        mesh=mesh,
        in_specs=placed,
        out_specs=P(None, ("groups", "gx", "gy"), None),
        check_vma=False,
    )
```

time: 1230 us -> 592 us (0.48)
  waiting for transfers between devices: 946 us -> 2.2 us
  Pallas kernels: 0 us -> 516 us
  starting transfers between devices: 93.4 us -> 0.13 us
  local copies, waits for them, and re-layouts: 67.9 us -> 6.16 us
  other arithmetic: 45.3 us -> 0.31 us
    pallas_call x0 -> x2, Pallas kernels: none -> 516 us  [the longest x1 270 us: dispatch(): pl.pallas_call(functools.partial(dispatch_kernel, ring), out_shape=(jax.S...]
    all_to_all x6 -> x0, waiting for transfers between devices: 507 us -> none  [the longest x2 312 us: body(): lax.all_to_all(half_rows, 'gx', split_axis=0, concat_axis=0, tiled=True)]
    ppermute x2 -> x0, waiting for transfers between devices: 439 us -> none  [swapped(): lax.ppermute(value, axis, [(i, i ^ 1 << stride) for i in range(lax.axis_s...]
    all_to_all x6 -> x0, starting transfers between devices: 90.6 us -> none  [the longest x4 47.9 us: several_exchanges(): lax.all_to_all(share, axis, split_axis=0, concat_axis=0, tiled=True)]
    unnamed x16 -> x15, local copies, waits for them, and re-layouts: 20.7 us -> 3 us
    reshape x6 -> x1, local copies, waits for them, and re-layouts: 17.1 us -> 0.08 us  [body(): gates = gate_weights.reshape(batches * rows, topk)]
    dot_general x12 -> x4, matrix products: 52 us -> 48.8 us  [the longest x2 38.7 us: body(): jnp.dot(hidden, full_down[q], preferred_element_type=jnp.float32)]
  transfers between devices with their start and end apart: 9 -> 3, of which waited for: 6 -> 0; matrix products, arithmetic and copies ran while one was open for 10% -> 2% of each run, Pallas kernels for 0% -> 46%
where the time goes in v1:
time: 592 us; the launch traced here: 587 us
  Pallas kernels  516 us (87%)
  matrix products  48.8 us (8%)
  between operations  13.6 us (2%)
  local copies, waits for them, and re-layouts  6.16 us (1%)
    pallas_call x1, Pallas kernels, dispatch(): pl.pallas_call(functools.partial(dispatch_kernel, ring), out_shape=(jax.S...  270 us
    pallas_call x1, Pallas kernels, give_back(): pl.pallas_call(functools.partial(return_kernel, ring), out_shape=jax.Shap...  246 us
    dot_general x2, matrix products, body(): jnp.dot(hidden, full_down[q], preferred_element_type=jnp.float32)  38.7 us
  transfers between devices with their start and end apart: 3, of which 0 were waited for; matrix products, arithmetic and copies ran while one was open for 2% of the time, Pallas kernels for 46%

profile of v1, /device:TPU:46, one launch (start us, length us, event | category | flops | bytes accessed | tf_op | source)
XLA Modules:
  0.0 586.8 jit_solution(4711850734770325912)
XLA Ops:
  6.6 0.0 all-gather.4.cloned.1.call-start
  6.6 0.7 all-gather.4.cloned.1.call-update
  7.3 0.1 all-gather.6.cloned.1.call-start
  7.4 0.7 all-gather.6.cloned.1.call-update
  8.1 0.1 all-gather.8.cloned.1.call-start
  8.2 0.7 all-gather.8.cloned.1.call-update
  8.9 0.0 copy-done.1
  8.9 0.1 copy.23
  9.0 0.1 eq.15
  9.1 0.1 iota_compare_fusion
  9.2 0.2 convert_reduce_fusion
  9.4 0.1 reduce_sum.12
  9.5 0.1 copy.24
  9.6 0.1 mul.33
  9.7 0.1 add.41
  9.8 0.1 add.42
  9.8 0.0 copy-done.2
  9.9 0.1 reshape.40
  10.0 0.6 pad.4.meta_ref
  10.6 269.8 %dispatch.1 = (bf16[512,7168]{1,0:T(8,128)(2,1)}, f32[2,16,8,128]{3,2,1,0:T(8,128)}) custom-call(bf16[64,7168]{1,0:T(8,128)(2,1)} %bitcast.49, f32[8,128]{1,0:T(8,128)} %pad.4.meta_ref), custom_call_target="tpu_custom_call" | custom-call | flops 939524096 | bytes 440401920 | tf_op jit(solution)/shard_map/dispatch/pallas_call | solution.py:323
  280.4 0.8 slice_bitcast_fusion.24
  281.2 0.0 slice-start
  281.2 1.1 copy.26
  282.3 7.2 %fusion.4 = f32[512,256]{1,0:T(8,128)} fusion(bf16[512,7168]{1,0:T(8,128)(2,1)} %get-tuple-element.7, bf16[2,7168,256]{2,1,0:T(8,128)(2,1)} %all-gather.4.cloned.1.call-done), kind=kOutput, calls=%fused_computation.11 | convolution fusion | flops 1879048192 | bytes 11534336 | tf_op jit(solution)/shard_map/dot_general | solution.py:405
  289.5 0.0 slice-done
  289.5 0.0 slice-done.1
  289.5 0.7 copy-done.3
  290.2 2.9 fusion.1
  293.1 18.4 %fusion.2 = f32[512,7168]{1,0:T(8,128)} fusion(bf16[2,256,7168]{2,1,0:T(8,128)(2,1)} %all-gather.8.cloned.1.call-done, bf16[512,7168]{1,0:T(8,128)(2,1)} %get-tuple-element.7, bf16[2,7168,256]{2,1,0:T(8,128)(2,1)} %all-gather.6.cloned.1.call-done, f32[512,256]{1,0:T(8,128)} %fusion.4), kind=kOutput, calls=%fused_computation.7 | convolution fusion | flops 3758882816 | bytes 29884416 | tf_op jit(solution)/shard_map/dot_general | solution.py:408
  311.5 20.4 %add_convert_fusion.y_ref = bf16[512,7168]{1,0:T(8,128)(2,1)} fusion(f32[512,7168]{1,0:T(8,128)} %fusion.2, bf16[2,256,7168]{2,1,0:T(8,128)(2,1)} %all-gather.8.cloned.1.call-done, bf16[512,7168]{1,0:T(8,128)(2,1)} %get-tuple-element.7, bf16[2,7168,256]{2,1,0:T(8,128)(2,1)} %all-gather.6.cloned.1.call-done, f32[512,256]{1,0:T(8,128)S(1)} %copy-done), kind=kOutput, calls=%fused_computation | convolution fusion | flops 3766222848 | bytes 37224448 | tf_op jit(solution)/shard_map/dot_general | solution.py:408
  331.9 245.8 %give_back.1 = bf16[64,7168]{1,0:T(8,128)(2,1)} custom-call(bf16[512,7168]{1,0:T(8,128)(2,1)} %add_convert_fusion.y_ref, f32[18,64,4]{2,1,0:T(8,128)} %bitcast.48), custom_call_target="tpu_custom_call" | custom-call | flops 939524096 | bytes 440401920 | tf_op jit(solution)/shard_map/give_back/pallas_call | solution.py:352
  577.6 2.2 copy.28
  (19 shorter events, 0.1 us)
Async XLA Ops:
  6.5 2.4 copy-start.1
  6.5 3.3 copy-start.2
  6.6 275.8 %all-gather.4.cloned.1.call-start = ((), (), s32[]{:S(2)}) async-start(), calls=%async_computation | async-start | bytes 11010048 | tf_op jit(solution)/shard_map/all_gather | solution.py:397
  7.3 285.8 %all-gather.6.cloned.1.call-start = ((), (), s32[]{:S(2)}) async-start(), calls=%async_computation.1 | async-start | bytes 11010048 | tf_op jit(solution)/shard_map/all_gather | solution.py:398
  8.1 285.0 %all-gather.8.cloned.1.call-start = ((), (), s32[]{:S(2)}) async-start(), calls=%async_computation.2 | async-start | bytes 11010048 | tf_op jit(solution)/shard_map/all_gather | solution.py:399
  281.2 8.3 %slice-start = ((s8[7340032]{0:T(1024)(128)(4,1)}), s8[3145728]{0:T(1024)(128)(4,1)S(1)}, s32[]{:S(2)}) async-start(s8[7340032]{0:T(1024)(128)(4,1)} %bitcast.45), calls=%async_computation.3 | async-start | bytes 6291456
  282.3 7.2 %slice-start.1 = ((s8[7340032]{0:T(1024)(128)(4,1)}), s8[4194304]{0:T(1024)(128)(4,1)S(1)}, s32[]{:S(2)}) async-start(s8[7340032]{0:T(1024)(128)(4,1)} %bitcast.45), calls=%async_computation.4 | async-start | bytes 8388608
  282.3 7.9 %copy-start.3 = (bf16[2,7168,256]{2,1,0:T(8,128)(2,1)S(1)}, bf16[2,7168,256]{2,1,0:T(8,128)(2,1)}, u32[]{:S(2)}) copy-start(bf16[2,7168,256]{2,1,0:T(8,128)(2,1)} %all-gather.4.cloned.1.call-done) | copy-start | bytes 22020100
  293.1 18.4 %copy-start = (f32[512,256]{1,0:T(8,128)S(1)}, f32[512,256]{1,0:T(8,128)}, u32[]{:S(2)}) copy-start(f32[512,256]{1,0:T(8,128)} %fusion.1) | copy-start | bytes 1572868
Sparse Core Ops, SparseCore 0:
  9.2 46.5 all-gather.3
  57.5 36.5 all-gather.5
  95.9 36.5 all-gather.7
